TPU v7x, 32 devices: a whole 2x2x4 slice. The times are simulated.
32 devices in a mesh: mode: 8 (over y, x, core), tm: 4 (over z).
Axes of the slice: x: 2, y: 2, z: 4, core: 2. Of those that a mesh axis runs over, the one named last changes fastest.
Arguments:
- field: float32 [2, 128, 65536], P(None, 'mode', 'tm'), may hold values from -1.8 to 1.8
- beta: float32 [3, 128], P(None, 'mode'), may hold values from -1 to 1
- quartets: int32 [4, 1024], replicated, may hold values from 0 to 127
- intersections: float32 [1024], replicated, may hold values from -0.12 to 0.12
Outputs:
- field_out: float32 [2, 128, 65536], P(None, 'mode', 'tm')
- errors: float32 [2, 128], P(None, 'mode')
All inputs are finite; a program needn't handle non-finite values.
Results may differ from a plain program's by a relative error of at most 0.0003.
Values sent between devices are 32-bit elements; how exact they have to be, the bound alone decides.
A program may use at most 128 MiB of HBM per device.

v0:
```python
import math
import jax
import jax.numpy as jnp
from jax import lax
from jax.sharding import PartitionSpec as P

RADIX = 256
STEPS = 2
epsilon = 1e-06


def phase_of(offset, slope, curve, frequency):
    return math.pi * offset + 300.0 * slope * frequency + 3000.0 * curve * frequency * frequency


def triple_product(left_field, middle_field, conj_field):
    prod_re = left_field[0] * middle_field[0] - left_field[1] * middle_field[1]
    prod_im = left_field[0] * middle_field[1] + left_field[1] * middle_field[0]
    out_re = prod_re * conj_field[0] + prod_im * conj_field[1]
    out_im = prod_im * conj_field[0] - prod_re * conj_field[1]
    return (out_re, out_im)


def contract(form, first_operand, second_operand):
    return jnp.einsum(form, first_operand, second_operand, precision=lax.Precision.HIGHEST)


def rotate(real_part, imag_part, angle):
    cosine = jnp.cos(angle)
    sine_part = jnp.sin(angle)
    return (real_part * cosine - imag_part * sine_part, real_part * sine_part + imag_part * cosine)


def dft_tables(length):
    positions = lax.iota(jnp.int32, length)
    product = positions[:, None] * positions[None, :] % length
    angle = -2.0 * math.pi / length * product.astype(jnp.float32)
    return (jnp.cos(angle), jnp.sin(angle))


def to_columns(state):
    return lax.all_to_all(state, "tm", split_axis=3, concat_axis=2, tiled=True)


def to_rows(state):
    return lax.all_to_all(state, "tm", split_axis=2, concat_axis=3, tiled=True)


def linear_step(state, beta, table_re, table_im):
    radix_size = table_re.shape[0]
    total_time = radix_size * radix_size
    cols_local = state.shape[3]
    tm_index = lax.axis_index("tm")
    head_re = contract("ka,mab->mkb", table_re, state[0]) - contract(
        "ka,mab->mkb", table_im, state[1]
    )
    head_im = contract("ka,mab->mkb", table_re, state[1]) + contract(
        "ka,mab->mkb", table_im, state[0]
    )
    column = tm_index * cols_local + lax.iota(jnp.int32, cols_local)
    row_position = lax.iota(jnp.int32, radix_size)
    twist = (
        -2.0
        * math.pi
        / total_time
        * (row_position[:, None] * column[None, :] % total_time).astype(jnp.float32)
    )
    head_re, head_im = rotate(head_re, head_im, twist[None])
    turned = lax.all_to_all(
        jnp.stack([head_re, head_im]), "tm", split_axis=2, concat_axis=3, tiled=True
    )
    spec_re = contract("mcb,kb->mck", turned[0], table_re) - contract(
        "mcb,kb->mck", turned[1], table_im
    )
    spec_im = contract("mcb,kb->mck", turned[1], table_re) + contract(
        "mcb,kb->mck", turned[0], table_im
    )
    rows_local = turned.shape[2]
    first_index = tm_index * rows_local + lax.iota(jnp.int32, rows_local)
    wave = first_index[:, None] + radix_size * row_position[None, :]
    signed = jnp.where(wave < total_time // 2, wave, wave - total_time)
    frequency = signed.astype(jnp.float32) / (total_time / 2)
    angle = phase_of(
        beta[0][:, None, None], beta[1][:, None, None], beta[2][:, None, None], frequency[None]
    )
    spec_re, spec_im = rotate(spec_re, spec_im, angle)
    back_re = contract("mck,kb->mcb", spec_re, table_re) + contract(
        "mck,kb->mcb", spec_im, table_im
    )
    back_im = contract("mck,kb->mcb", spec_im, table_re) - contract(
        "mck,kb->mcb", spec_re, table_im
    )
    untwist = (
        2.0
        * math.pi
        / total_time
        * (first_index[:, None] * row_position[None, :] % total_time).astype(jnp.float32)
    )
    back_re, back_im = rotate(back_re, back_im, untwist[None])
    gathered = lax.all_to_all(
        jnp.stack([back_re, back_im]), "tm", split_axis=3, concat_axis=2, tiled=True
    )
    scale = 1.0 / total_time
    out_re = (
        contract("ka,mkb->mab", table_re, gathered[0])
        + contract("ka,mkb->mab", table_im, gathered[1])
    ) * scale
    out_im = (
        contract("ka,mkb->mab", table_re, gathered[1])
        - contract("ka,mkb->mab", table_im, gathered[0])
    ) * scale
    return jnp.stack([out_re, out_im])


def kerr_term(fields, quartets, intersections):
    count = quartets.shape[1]
    block_size = min(512, count)
    blocks = count // block_size
    grouped = quartets.reshape(4, blocks, block_size).transpose(1, 0, 2)
    weights = intersections.reshape(blocks, block_size)
    modes_all = fields.shape[1]
    mode_ids = lax.iota(jnp.int32, modes_all)

    def accumulate(running, block_item):
        indices, weight = block_item
        out_re, out_im = triple_product(
            jnp.take(fields, indices[1], axis=1),
            jnp.take(fields, indices[2], axis=1),
            jnp.take(fields, indices[3], axis=1),
        )
        owner = (indices[0][None, :] == mode_ids[:, None]).astype(jnp.float32) * weight[None, :]
        add_re = contract("pq,qt->pt", owner, -out_im)
        add_im = contract("pq,qt->pt", owner, out_re)
        return (running + jnp.stack([add_re, add_im]), None)

    running, unused = lax.scan(accumulate, jnp.zeros_like(fields), (grouped, weights))
    return running


def kerr_step(flat, quartets, intersections):
    spread = lax.all_to_all(flat, "mode", split_axis=2, concat_axis=1, tiled=True)
    first = kerr_term(spread, quartets, intersections)
    second = kerr_term(spread + first, quartets, intersections)
    updated = spread + 0.5 * (first + second)
    estimate = 0.5 * (second - first)
    returned, estimate_home = (
        lax.all_to_all(updated, "mode", split_axis=1, concat_axis=2, tiled=True),
        lax.all_to_all(estimate, "mode", split_axis=1, concat_axis=2, tiled=True),
    )
    error_part = jnp.sum(estimate_home * estimate_home, axis=(0, 2))
    field_part = jnp.sum(returned * returned, axis=(0, 2))
    return (returned, error_part, field_part)


def shards(field, beta, quartets, intersections):
    modes_local = field.shape[1]
    time_local = field.shape[2]
    table_re, table_im = dft_tables(RADIX)
    state = field.reshape(2, modes_local, time_local // RADIX, RADIX)
    state = to_columns(state)
    error_rows = []
    for step_index in range(STEPS):
        columns = state
        columns = linear_step(columns, beta, table_re, table_im)
        updated, error_part, field_part = kerr_step(
            columns.reshape(2, modes_local, time_local), quartets, intersections
        )
        error_sq, field_sq = lax.psum((error_part, field_part), "tm")
        error_rows.append(jnp.sqrt(error_sq / (field_sq + epsilon)))
        state = updated.reshape(columns.shape)
    state = to_rows(state)
    errors = jnp.stack(error_rows)
    return (state.reshape(2, modes_local, time_local), errors)


def solution(mesh):
    placed = (P(None, "mode", "tm"), P(None, "mode"), P(), P())
    return jax.shard_map(
        shards,
        mesh=mesh,
        in_specs=placed,
        out_specs=(P(None, "mode", "tm"), P(None, "mode")),
        check_vma=False,
    )
```

profile of v0, /device:TPU:18, one launch (start us, length us, event | category | flops | bytes accessed | tf_op | source)
XLA Modules:
  0.0 1882.4 jit_solution(8491664908036585077)
XLA Ops:
  18.4 44.6 %all-to-all-done = f32[4,1,131072]{2,1,0:T(1,128)S(1)} async-done(((f32[4,1,131072]{2,1,0:T(1,128)}), f32[4,1,131072]{2,1,0:T(1,128)S(1)}, u32[]{:S(2)}, u32[]{:S(2)}) %all-to-all-start) | async-done | bytes 2097184 | tf_op jit(solution)/shard_map/all_to_all | solution.py:42
  133.5 44.1 %all-to-all-done.1 = f32[4,1,131072]{2,1,0:T(1,128)} async-done(((f32[4,1,131072]{2,1,0:T(1,128)}), f32[4,1,131072]{2,1,0:T(1,128)}, u32[]{:S(2)}, u32[]{:S(2)}) %all-to-all-start.1) | async-done | bytes 2097184 | tf_op jit(solution)/shard_map/all_to_all | solution.py:69
  231.1 51.6 %all_to_all.174 = f32[4,1,131072]{2,1,0:T(1,128)} all-to-all(f32[4,1,131072]{2,1,0:T(1,128)S(1)} %reshape.495), channel_id=1, replica_groups=mesh['mode'=8,'tm'=4] {'tm'}, dimensions={0} | all-to-all | bytes 4194304 | tf_op jit(solution)/shard_map/all_to_all | solution.py:100
  337.0 24.7 %reshape.497 = f32[8,1,65536]{2,1,0:T(1,128)} reshape(f32[16384,2,16]{2,1,0:T(2,128)} %bitcast.446) | data formatting | bytes 4194304
  366.8 25.0 %all-to-all-done.3 = f32[8,1,65536]{2,1,0:T(1,128)} async-done(((f32[8,1,65536]{2,1,0:T(1,128)}), f32[8,1,65536]{2,1,0:T(1,128)}, u32[]{:S(2)}, u32[]{:S(2)}) %all-to-all-start.3) | async-done | bytes 2097184 | tf_op jit(solution)/shard_map/all_to_all | solution.py:141
  399.1 28.6 %reshape.498 = f32[16384,2,16]{2,1,0:T(2,128)} reshape(f32[8,65536]{1,0:T(8,128)S(1)} %reduce.13) | data formatting | bytes 4194304
  427.7 21.6 %copy.201 = f32[2,16,8,2048]{3,1,2,0:T(8,128)} copy(f32[2,16,8,2048]{1,0,3,2:T(2,128)} %bitcast.447) | data formatting | bytes 4194304 | tf_op jit(solution)/shard_map/all_to_all | solution.py:141
  452.5 210.8 %while.44 = (s32[]{:T(128)}, f32[2,128,2048]{2,1,0:T(8,128)}, s32[2,4,512]{2,1,0:T(4,128)S(1)}, f32[2,512]{1,0:T(2,128)S(1)}, f32[2,128,2048]{2,0,1:T(2,128)S(1)}, /*index=5*/s32[]{:T(128)}, s32[]{:T(128)}, s32[]{}, s32[]{}, s32[]{}) while((s32[]{:T(128)}, f32[2,128,2048]{2,1,0:T(8,128)}, s32[2,4,512]{2,1,0:T(4,128)S(1)}, ...), condition=%wide.region_1.3_spmd.clone, body=%wide.region_0.2_spmd.clone.sunk | while | flops 3243000320 | bytes 234956048 | solution.py:136
  484.7 19.5 %gather_fusion.1 = f32[512,2,2048]{2,1,0:T(2,128)} fusion(f32[2,128,2048]{2,0,1:T(2,128)S(1)} %get-tuple-element.665, s32[1024]{0:T(1024)S(1)} %pad_clamp_fusion.25), kind=kCustom, calls=%fused_computation.clone.clone.1 | custom fusion | bytes 16779264 | tf_op jit(solution)/shard_map/while/body/eval_jaxpr/jit(_take)/gather | solution.py:127
  517.7 19.7 %gather_fusion.2 = f32[512,2,2048]{2,1,0:T(2,128)} fusion(f32[2,128,2048]{2,0,1:T(2,128)S(1)} %get-tuple-element.665, s32[1024]{0:T(1024)S(1)} %pad_clamp_fusion.26), kind=kCustom, calls=%fused_computation.2.clone.clone.1 | custom fusion | bytes 16779264 | tf_op jit(solution)/shard_map/while/body/eval_jaxpr/jit(_take)/gather | solution.py:129
  588.5 19.8 %gather_fusion.1 = f32[512,2,2048]{2,1,0:T(2,128)} fusion(f32[2,128,2048]{2,0,1:T(2,128)S(1)} %get-tuple-element.665, s32[1024]{0:T(1024)S(1)} %pad_clamp_fusion.25), kind=kCustom, calls=%fused_computation.clone.clone.1 | custom fusion | bytes 16779264 | tf_op jit(solution)/shard_map/while/body/eval_jaxpr/jit(_take)/gather | solution.py:127
  667.4 215.6 %while.45 = (s32[]{:T(128)}, f32[2,128,2048]{2,1,0:T(8,128)}, s32[2,4,512]{2,1,0:T(4,128)S(1)}, f32[2,512]{1,0:T(2,128)S(1)}, f32[2,128,2048]{2,0,1:T(2,128)S(1)}, /*index=5*/s32[]{:T(128)}, s32[]{:T(128)}, s32[]{}, s32[]{}, s32[]{}) while((s32[]{:T(128)}, f32[2,128,2048]{2,1,0:T(8,128)}, s32[2,4,512]{2,1,0:T(4,128)S(1)}, ...), condition=%wide.region_3.5_spmd.clone, body=%wide.region_2.4_spmd.clone.sunk | while | flops 3243000320 | bytes 234956048 | solution.py:136
  702.6 19.8 %gather_fusion.4 = f32[512,2,2048]{2,1,0:T(2,128)} fusion(f32[2,128,2048]{2,0,1:T(2,128)S(1)} %get-tuple-element.695, s32[1024]{0:T(1024)S(1)} %pad_clamp_fusion.28), kind=kCustom, calls=%fused_computation.3.clone.clone.1 | custom fusion | bytes 16779264 | tf_op jit(solution)/shard_map/while/body/eval_jaxpr/jit(_take)/gather | solution.py:127
  806.5 19.5 %gather_fusion.4 = f32[512,2,2048]{2,1,0:T(2,128)} fusion(f32[2,128,2048]{2,0,1:T(2,128)S(1)} %get-tuple-element.695, s32[1024]{0:T(1024)S(1)} %pad_clamp_fusion.28), kind=kCustom, calls=%fused_computation.3.clone.clone.1 | custom fusion | bytes 16779264 | tf_op jit(solution)/shard_map/while/body/eval_jaxpr/jit(_take)/gather | solution.py:127
  839.5 19.7 %gather_fusion.5 = f32[512,2,2048]{2,1,0:T(2,128)} fusion(f32[2,128,2048]{2,0,1:T(2,128)S(1)} %get-tuple-element.695, s32[1024]{0:T(1024)S(1)} %pad_clamp_fusion.29), kind=kCustom, calls=%fused_computation.5.clone.clone.1 | custom fusion | bytes 16779264 | tf_op jit(solution)/shard_map/while/body/eval_jaxpr/jit(_take)/gather | solution.py:129
  889.7 29.1 %all_to_all.175 = f32[2,128,2048]{2,0,1:T(2,128)S(1)} all-to-all(f32[2,128,2048]{2,0,1:T(2,128)S(1)} %copy.171), channel_id=1, replica_groups=mesh['mode'=8,'tm'=4] {'mode'}, dimensions={1} | all-to-all | bytes 4194304 | tf_op jit(solution)/shard_map/all_to_all | solution.py:147
  956.1 51.8 %all_to_all.176 = f32[4,1,131072]{2,1,0:T(1,128)} all-to-all(f32[4,1,131072]{2,1,0:T(1,128)S(1)} %reshape.499), channel_id=1, replica_groups=mesh['mode'=8,'tm'=4] {'tm'}, dimensions={0} | all-to-all | bytes 4194304 | tf_op jit(solution)/shard_map/all_to_all | solution.py:69
  1061.5 51.0 %all_to_all.177 = f32[4,1,131072]{2,1,0:T(1,128)} all-to-all(f32[4,1,131072]{2,1,0:T(1,128)S(1)} %reshape.501), channel_id=1, replica_groups=mesh['mode'=8,'tm'=4] {'tm'}, dimensions={0} | all-to-all | bytes 4194304 | tf_op jit(solution)/shard_map/all_to_all | solution.py:100
  1166.4 24.8 %reshape.503 = f32[8,1,65536]{2,1,0:T(1,128)} reshape(f32[16384,2,16]{2,1,0:T(2,128)} %bitcast.448) | data formatting | bytes 4194304
  1198.9 22.2 %all-to-all-done.7 = f32[8,1,65536]{2,1,0:T(1,128)} async-done(((f32[8,1,65536]{2,1,0:T(1,128)}), f32[8,1,65536]{2,1,0:T(1,128)}, u32[]{:S(2)}, u32[]{:S(2)}) %all-to-all-start.7) | async-done | bytes 2097184 | tf_op jit(solution)/shard_map/all_to_all | solution.py:141
  1234.4 28.7 %reshape.504 = f32[16384,2,16]{2,1,0:T(2,128)} reshape(f32[8,65536]{1,0:T(8,128)S(1)} %reduce.16) | data formatting | bytes 4194304
  1263.1 21.6 %copy.203 = f32[2,16,8,2048]{3,1,2,0:T(8,128)} copy(f32[2,16,8,2048]{1,0,3,2:T(2,128)} %bitcast.449) | data formatting | bytes 4194304 | tf_op jit(solution)/shard_map/all_to_all | solution.py:141
  1288.0 210.6 %while.46 = (s32[]{:T(128)}, f32[2,128,2048]{2,1,0:T(8,128)}, s32[2,4,512]{2,1,0:T(4,128)S(1)}, f32[2,512]{1,0:T(2,128)S(1)}, f32[2,128,2048]{2,0,1:T(2,128)S(1)}, /*index=5*/s32[]{:T(128)}, s32[]{:T(128)}, s32[]{}, s32[]{}, s32[]{}) while((s32[]{:T(128)}, f32[2,128,2048]{2,1,0:T(8,128)}, s32[2,4,512]{2,1,0:T(4,128)S(1)}, ...), condition=%wide.region_5.7_spmd.clone, body=%wide.region_4.6_spmd.clone.sunk | while | flops 3243000320 | bytes 234956048 | solution.py:136
  1320.0 19.8 %gather_fusion.7 = f32[512,2,2048]{2,1,0:T(2,128)} fusion(f32[2,128,2048]{2,0,1:T(2,128)S(1)} %get-tuple-element.725, s32[1024]{0:T(1024)S(1)} %pad_clamp_fusion.31), kind=kCustom, calls=%fused_computation.6.clone.clone.1 | custom fusion | bytes 16779264 | tf_op jit(solution)/shard_map/while/body/eval_jaxpr/jit(_take)/gather | solution.py:127
  1424.0 19.5 %gather_fusion.7 = f32[512,2,2048]{2,1,0:T(2,128)} fusion(f32[2,128,2048]{2,0,1:T(2,128)S(1)} %get-tuple-element.725, s32[1024]{0:T(1024)S(1)} %pad_clamp_fusion.31), kind=kCustom, calls=%fused_computation.6.clone.clone.1 | custom fusion | bytes 16779264 | tf_op jit(solution)/shard_map/while/body/eval_jaxpr/jit(_take)/gather | solution.py:127
  1456.9 19.7 %gather_fusion.8 = f32[512,2,2048]{2,1,0:T(2,128)} fusion(f32[2,128,2048]{2,0,1:T(2,128)S(1)} %get-tuple-element.725, s32[1024]{0:T(1024)S(1)} %pad_clamp_fusion.32), kind=kCustom, calls=%fused_computation.8.clone.clone.1 | custom fusion | bytes 16779264 | tf_op jit(solution)/shard_map/while/body/eval_jaxpr/jit(_take)/gather | solution.py:129
  1502.7 229.3 %while.47 = (s32[]{:T(128)}, f32[2,128,2048]{2,1,0:T(8,128)}, s32[2,4,512]{2,1,0:T(4,128)S(1)}, f32[2,512]{1,0:T(2,128)S(1)}, f32[2,128,2048]{2,0,1:T(2,128)S(1)}, /*index=5*/s32[]{:T(128)}, s32[]{:T(128)}, s32[]{}, s32[]{}, s32[]{}) while((s32[]{:T(128)}, f32[2,128,2048]{2,1,0:T(8,128)}, s32[2,4,512]{2,1,0:T(4,128)S(1)}, ...), condition=%wide.region_7.9_spmd.clone, body=%wide.region_6.8_spmd.clone.sunk | while | flops 3243000320 | bytes 234956048 | solution.py:136
  1538.0 30.0 %gather_fusion.10 = f32[512,2,2048]{2,1,0:T(2,128)} fusion(f32[2,128,2048]{2,0,1:T(2,128)S(1)} %get-tuple-element.755, s32[1024]{0:T(1024)S(1)} %pad_clamp_fusion.34), kind=kCustom, calls=%fused_computation.9.clone.clone.1 | custom fusion | bytes 16779264 | tf_op jit(solution)/shard_map/while/body/eval_jaxpr/jit(_take)/gather | solution.py:127
  1581.4 19.7 %gather_fusion.11 = f32[512,2,2048]{2,1,0:T(2,128)} fusion(f32[2,128,2048]{2,0,1:T(2,128)S(1)} %get-tuple-element.755, s32[1024]{0:T(1024)S(1)} %pad_clamp_fusion.35), kind=kCustom, calls=%fused_computation.11.clone.clone.1 | custom fusion | bytes 16779264 | tf_op jit(solution)/shard_map/while/body/eval_jaxpr/jit(_take)/gather | solution.py:129
  1652.1 19.7 %gather_fusion.10 = f32[512,2,2048]{2,1,0:T(2,128)} fusion(f32[2,128,2048]{2,0,1:T(2,128)S(1)} %get-tuple-element.755, s32[1024]{0:T(1024)S(1)} %pad_clamp_fusion.34), kind=kCustom, calls=%fused_computation.9.clone.clone.1 | custom fusion | bytes 16779264 | tf_op jit(solution)/shard_map/while/body/eval_jaxpr/jit(_take)/gather | solution.py:127
  1748.7 20.6 %all-to-all-done.8 = f32[2,128,2048]{2,0,1:T(2,128)S(1)} async-done(((f32[2,128,2048]{2,0,1:T(2,128)}), f32[2,128,2048]{2,0,1:T(2,128)S(1)}, u32[]{:S(2)}, u32[]{:S(2)}) %all-to-all-start.8) | async-done | bytes 2097184 | tf_op jit(solution)/shard_map/all_to_all | solution.py:147
  1817.5 39.8 %all-reduce = (f32[16]{0:T(128)S(1)}, f32[16]{0:T(128)S(1)}, f32[16]{0:T(128)S(1)}, f32[16]{0:T(128)S(1)}) all-reduce(f32[16]{0:T(128)S(1)} %reduce_sum.56, f32[16]{0:T(128)S(1)} %multiply_reduce_fusion, f32[16]{0:T(128)S(1)} %reduce_sum.52, f32[16]{0:T(128)S(1)} %multiply_reduce_fusion.2), channel_id=1, replica_groups=mesh['mode'=8,'tm'=4] {'tm'}, use_global_device_ids=true, to_apply=%region_15.17 | all-reduce | flops 64 | bytes 512 | tf_op jit(solution)/shard_map/psum | solution.py:168
  (396 shorter events, 1078.4 us)
Async XLA Ops:
  12.9 50.1 %all-to-all-start = ((f32[4,1,131072]{2,1,0:T(1,128)}), f32[4,1,131072]{2,1,0:T(1,128)S(1)}, u32[]{:S(2)}, u32[]{:S(2)}) async-start(f32[4,1,131072]{2,1,0:T(1,128)} %reshape.491), calls=%async_computation | async-start | bytes 4194304 | tf_op jit(solution)/shard_map/all_to_all | solution.py:42
  18.4 86.7 %copy-start.27 = (f32[256,64]{0,1:T(8,128)}, f32[256,64]{0,1:T(8,128)S(1)}, u32[]{:S(2)}) copy-start(f32[256,64]{0,1:T(8,128)S(1)} %get-tuple-element.433) | copy-start | bytes 196612
  18.4 86.7 %copy-start.29 = (f32[256,64]{0,1:T(8,128)}, f32[256,64]{0,1:T(8,128)S(1)}, u32[]{:S(2)}) copy-start(f32[256,64]{0,1:T(8,128)S(1)} %get-tuple-element.434) | copy-start | bytes 196612
  119.9 13.2 copy-start.40
  125.4 52.2 %all-to-all-start.1 = ((f32[4,1,131072]{2,1,0:T(1,128)}), f32[4,1,131072]{2,1,0:T(1,128)}, u32[]{:S(2)}, u32[]{:S(2)}) async-start(f32[4,1,131072]{2,1,0:T(1,128)} %reshape.493), calls=%async_computation.1 | async-start | bytes 4194304 | tf_op jit(solution)/shard_map/all_to_all | solution.py:69
  133.1 74.7 %copy-start.33 = (f32[16]{0:T(128)}, f32[16]{0:T(128)S(1)}, u32[]{:S(2)}) copy-start(f32[16]{0:T(128)S(1)} %get-tuple-element.427) | copy-start | bytes 196
  133.1 74.7 %copy-start.35 = (f32[16]{0:T(128)}, f32[16]{0:T(128)S(1)}, u32[]{:S(2)}) copy-start(f32[16]{0:T(128)S(1)} %get-tuple-element.428) | copy-start | bytes 196
  133.1 74.7 %copy-start.37 = (f32[16]{0:T(128)}, f32[16]{0:T(128)S(1)}, u32[]{:S(2)}) copy-start(f32[16]{0:T(128)S(1)} %get-tuple-element.429) | copy-start | bytes 196
  133.5 74.3 %copy-start.25 = (f32[64,256]{1,0:T(8,128)}, f32[64,256]{1,0:T(8,128)S(1)}, u32[]{:S(2)}) copy-start(f32[64,256]{1,0:T(8,128)S(1)} %get-tuple-element.432) | copy-start | bytes 196612
  133.5 86.2 %copy-start.21 = (f32[64,256]{1,0:T(8,128)}, f32[64,256]{1,0:T(8,128)S(1)}, u32[]{:S(2)}) copy-start(f32[64,256]{1,0:T(8,128)S(1)} %get-tuple-element.430) | copy-start | bytes 196612
  133.5 86.2 %copy-start.23 = (f32[64,256]{1,0:T(8,128)}, f32[64,256]{1,0:T(8,128)S(1)}, u32[]{:S(2)}) copy-start(f32[64,256]{1,0:T(8,128)S(1)} %get-tuple-element.431) | copy-start | bytes 196612
  361.7 30.1 %all-to-all-start.3 = ((f32[8,1,65536]{2,1,0:T(1,128)}), f32[8,1,65536]{2,1,0:T(1,128)}, u32[]{:S(2)}, u32[]{:S(2)}) async-start(f32[8,1,65536]{2,1,0:T(1,128)} %reshape.497), calls=%async_computation.3 | async-start | bytes 4194304 | tf_op jit(solution)/shard_map/all_to_all | solution.py:141
  537.4 9.2 copy-start
  537.5 9.2 copy-start.1
  641.2 9.2 copy-start
  641.2 9.2 copy-start.1
  755.3 9.2 copy-start.2
  755.4 9.2 copy-start.3
  859.2 9.2 copy-start.2
  859.2 9.2 copy-start.3
  930.9 11.7 copy-start.28
  930.9 11.7 copy-start.30
  1191.2 29.9 %all-to-all-start.7 = ((f32[8,1,65536]{2,1,0:T(1,128)}), f32[8,1,65536]{2,1,0:T(1,128)}, u32[]{:S(2)}, u32[]{:S(2)}) async-start(f32[8,1,65536]{2,1,0:T(1,128)} %reshape.503), calls=%async_computation.7 | async-start | bytes 4194304 | tf_op jit(solution)/shard_map/all_to_all | solution.py:141
  1221.1 518.9 %all-to-all-start.10 = ((f32[2,128,2048]{2,0,1:T(2,128)}), f32[2,128,2048]{2,0,1:T(2,128)}, u32[]{:S(2)}, u32[]{:S(2)}) async-start(f32[2,128,2048]{2,0,1:T(2,128)} %copy.193), calls=%async_computation.10 | async-start | bytes 4194304 | tf_op jit(solution)/shard_map/all_to_all | solution.py:148
  1476.6 9.2 copy-start.4
  1476.6 9.2 copy-start.5
  1704.7 9.2 copy-start.6
  1704.7 9.2 copy-start.7
  1739.9 29.3 %all-to-all-start.8 = ((f32[2,128,2048]{2,0,1:T(2,128)}), f32[2,128,2048]{2,0,1:T(2,128)S(1)}, u32[]{:S(2)}, u32[]{:S(2)}) async-start(f32[2,128,2048]{2,0,1:T(2,128)} %copy.188), calls=%async_computation.8 | async-start | bytes 4194304 | tf_op jit(solution)/shard_map/all_to_all | solution.py:147
  1769.3 31.0 %all-to-all-start.11 = ((f32[2,128,2048]{2,0,1:T(2,128)}), f32[2,128,2048]{2,0,1:T(2,128)}, u32[]{:S(2)}, u32[]{:S(2)}) async-start(f32[2,128,2048]{2,0,1:T(2,128)} %copy.194), calls=%async_computation.11 | async-start | bytes 4194304 | tf_op jit(solution)/shard_map/all_to_all | solution.py:148
  1794.5 16.0 copy-start.14
  1800.2 57.6 %all-to-all-start.9 = ((f32[4,1,131072]{2,1,0:T(1,128)}), f32[4,1,131072]{2,1,0:T(1,128)}, u32[]{:S(2)}, u32[]{:S(2)}) async-start(f32[4,1,131072]{2,1,0:T(1,128)} %reshape.505), calls=%async_computation.9 | async-start | bytes 4194304 | tf_op jit(solution)/shard_map/all_to_all | solution.py:46
  (29 other events, 197.8 us)
where the time goes:
time: 1890 us; the launch traced here: 1880 us
  local copies, waits for them, and re-layouts  878 us (46%)
  other arithmetic  397 us (21%)
  blocking collectives  223 us (12%)
  waiting for transfers between devices  162 us (9%)
  matrix products  148 us (8%)
  starting transfers between devices  46.1 us (2%)
  loops' own time  25.8 us (1%)
    unnamed x79, local copies, waits for them, and re-layouts  174 us
    gather x8, local copies, waits for them, and re-layouts, accumulate(): jnp.take(fields, indices[1], axis=1)  168 us
    gather x8, local copies, waits for them, and re-layouts, accumulate(): jnp.take(fields, indices[3], axis=1)  157 us
    gather x8, local copies, waits for them, and re-layouts, accumulate(): jnp.take(fields, indices[2], axis=1)  155 us
    dot_general x44, matrix products, contract(): jnp.einsum(form, first_operand, second_operand, precision=lax.Precision.H...  138 us
    all_to_all x2, blocking collectives, linear_step(): lax.all_to_all(jnp.stack([back_re, back_im]), 'tm', split_axis=3, concat_...  103 us
    select_n x8, other arithmetic, accumulate(): jnp.take(fields, indices[2], axis=1)  99.3 us
    select_n x16, other arithmetic, accumulate(): jnp.take(fields, indices[3], axis=1)  73.6 us
  transfers between devices with their start and end apart: 8, of which 6 were waited for; matrix products, arithmetic and copies ran while one was open for 28% of the time, Pallas kernels for 0%

commit v1 on v0

--- a/solution.py
+++ b/solution.py
@@ -138,7 +138,15 @@
 
 
 def kerr_step(flat, quartets, intersections):
-    spread = lax.all_to_all(flat, "mode", split_axis=2, concat_axis=1, tiled=True)
+    ways, here = (lax.axis_size("mode"), lax.axis_index("mode"))
+    width = flat.shape[2] // ways
+    turned_2 = jnp.roll(flat, -here * width, axis=2)
+    got = [lax.slice_in_dim(turned_2, 0, width, axis=2)]
+    for far in range(1, ways):
+        sent = lax.slice_in_dim(turned_2, far * width, (far + 1) * width, axis=2)
+        got.append(lax.ppermute(sent, "mode", [(d, (d + far) % ways) for d in range(ways)]))
+    line = jnp.concatenate(got[::-1], axis=1)
+    spread = jnp.roll(line, (here + 1) * got[0].shape[1], axis=1)
     first = kerr_term(spread, quartets, intersections)
     second = kerr_term(spread + first, quartets, intersections)
     updated = spread + 0.5 * (first + second)

time: 1890 us -> 1730 us (0.915)
  local copies, waits for them, and re-layouts: 878 us -> 701 us
  blocking collectives: 223 us -> 174 us
  waiting for transfers between devices: 162 us -> 211 us
  starting transfers between devices: 46.1 us -> 73.7 us
    unnamed x79 -> x95, local copies, waits for them, and re-layouts: 174 us -> 71.8 us
    all_to_all x2 -> x1, blocking collectives: 103 us -> 51 us  [linear_step(): lax.all_to_all(jnp.stack([back_re, back_im]), 'tm', split_axis=3, concat_...]
    ppermute x0 -> x14, waiting for transfers between devices: none -> 51.5 us  [kerr_step(): lax.ppermute(sent, 'mode', [(d, (d + far) % ways) for d in range(ways)])]
    all_to_all x2 -> x0, local copies, waits for them, and re-layouts: 43.2 us -> none  [kerr_step(): lax.all_to_all(flat, 'mode', split_axis=2, concat_axis=1, tiled=True)]
    another operation x6 -> x4, local copies, waits for them, and re-layouts: 34.2 us -> 6.61 us  [linear_step(): return jnp.stack([out_re, out_im])]
    all_to_all x2 -> x1, waiting for transfers between devices: 47.2 us -> 44.3 us  [linear_step(): lax.all_to_all(jnp.stack([back_re, back_im]), 'tm', split_axis=3, concat_...]
  transfers between devices with their start and end apart: 8 -> 21, of which waited for: 6 -> 13; matrix products, arithmetic and copies ran while one was open for 28% -> 27% of each run, Pallas kernels for 0% -> 0%
where the time goes in v1:
time: 1730 us; the launch traced here: 1720 us
  local copies, waits for them, and re-layouts  701 us (41%)
  other arithmetic  384 us (22%)
  waiting for transfers between devices  211 us (12%)
  blocking collectives  174 us (10%)
  matrix products  151 us (9%)
  starting transfers between devices  73.7 us (4%)
  loops' own time  26.1 us (2%)
    gather x8, local copies, waits for them, and re-layouts, accumulate(): jnp.take(fields, indices[1], axis=1)  167 us
    gather x8, local copies, waits for them, and re-layouts, accumulate(): jnp.take(fields, indices[3], axis=1)  157 us
    gather x8, local copies, waits for them, and re-layouts, accumulate(): jnp.take(fields, indices[2], axis=1)  154 us
    dot_general x44, matrix products, contract(): jnp.einsum(form, first_operand, second_operand, precision=lax.Precision.H...  141 us
    select_n x8, other arithmetic, accumulate(): jnp.take(fields, indices[2], axis=1)  99 us
    select_n x16, other arithmetic, accumulate(): jnp.take(fields, indices[3], axis=1)  73.6 us
    select_n x16, other arithmetic, accumulate(): jnp.take(fields, indices[1], axis=1)  73.6 us
    unnamed x95, local copies, waits for them, and re-layouts  71.8 us
  transfers between devices with their start and end apart: 21, of which 13 were waited for; matrix products, arithmetic and copies ran while one was open for 27% of the time, Pallas kernels for 0%

profile of v1, /device:TPU:18, one launch (start us, length us, event | category | flops | bytes accessed | tf_op | source)
XLA Modules:
  0.0 1722.5 jit_solution(17332745062665443782)
XLA Ops:
  18.4 44.6 %all-to-all-done = f32[4,1,131072]{2,1,0:T(1,128)S(1)} async-done(((f32[4,1,131072]{2,1,0:T(1,128)}), f32[4,1,131072]{2,1,0:T(1,128)S(1)}, u32[]{:S(2)}, u32[]{:S(2)}) %all-to-all-start) | async-done | bytes 2097184 | tf_op jit(solution)/shard_map/all_to_all | solution.py:42
  124.2 44.1 %all-to-all-done.1 = f32[4,1,131072]{2,1,0:T(1,128)} async-done(((f32[4,1,131072]{2,1,0:T(1,128)}), f32[4,1,131072]{2,1,0:T(1,128)}, u32[]{:S(2)}, u32[]{:S(2)}) %all-to-all-start.1) | async-done | bytes 2097184 | tf_op jit(solution)/shard_map/all_to_all | solution.py:69
  230.6 44.3 %all-to-all-done.2 = f32[4,1,131072]{2,1,0:T(1,128)} async-done(((f32[4,1,131072]{2,1,0:T(1,128)}), f32[4,1,131072]{2,1,0:T(1,128)}, u32[]{:S(2)}, u32[]{:S(2)}) %all-to-all-start.2) | async-done | bytes 2097184 | tf_op jit(solution)/shard_map/all_to_all | solution.py:100
  348.3 210.7 %while.44 = (s32[]{:T(128)}, f32[2,128,2048]{2,1,0:T(8,128)}, s32[2,4,512]{2,1,0:T(4,128)S(1)}, f32[2,512]{1,0:T(2,128)S(1)}, f32[2,128,2048]{2,0,1:T(2,128)S(1)}, /*index=5*/s32[]{:T(128)}, s32[]{:T(128)}, s32[]{}, s32[]{}, s32[]{}) while((s32[]{:T(128)}, f32[2,128,2048]{2,1,0:T(8,128)}, s32[2,4,512]{2,1,0:T(4,128)S(1)}, ...), condition=%wide.region_1.5_spmd.clone, body=%wide.region_0.4_spmd.clone.sunk | while | flops 3243000320 | bytes 234956048 | solution.py:136
  380.2 19.7 %gather_fusion.1 = f32[512,2,2048]{2,1,0:T(2,128)} fusion(f32[2,128,2048]{2,0,1:T(2,128)S(1)} %get-tuple-element.681, s32[1024]{0:T(1024)S(1)} %pad_clamp_fusion.25), kind=kCustom, calls=%fused_computation.clone.clone.1 | custom fusion | bytes 16779264 | tf_op jit(solution)/shard_map/while/body/eval_jaxpr/jit(_take)/gather | solution.py:127
  413.3 19.5 %gather_fusion.2 = f32[512,2,2048]{2,1,0:T(2,128)} fusion(f32[2,128,2048]{2,0,1:T(2,128)S(1)} %get-tuple-element.681, s32[1024]{0:T(1024)S(1)} %pad_clamp_fusion.26), kind=kCustom, calls=%fused_computation.2.clone.clone.1 | custom fusion | bytes 16779264 | tf_op jit(solution)/shard_map/while/body/eval_jaxpr/jit(_take)/gather | solution.py:129
  452.3 19.3 %gather_fusion = f32[512,2,2048]{2,1,0:T(2,128)} fusion(f32[2,128,2048]{2,0,1:T(2,128)S(1)} %get-tuple-element.681, s32[1024]{0:T(1024)S(1)} %pad_clamp_fusion.24), kind=kCustom, calls=%fused_computation.1.clone.clone.1 | custom fusion | bytes 16779264 | tf_op jit(solution)/shard_map/while/body/eval_jaxpr/jit(_take)/gather | solution.py:128
  484.0 19.5 %gather_fusion.1 = f32[512,2,2048]{2,1,0:T(2,128)} fusion(f32[2,128,2048]{2,0,1:T(2,128)S(1)} %get-tuple-element.681, s32[1024]{0:T(1024)S(1)} %pad_clamp_fusion.25), kind=kCustom, calls=%fused_computation.clone.clone.1 | custom fusion | bytes 16779264 | tf_op jit(solution)/shard_map/while/body/eval_jaxpr/jit(_take)/gather | solution.py:127
  516.9 19.8 %gather_fusion.2 = f32[512,2,2048]{2,1,0:T(2,128)} fusion(f32[2,128,2048]{2,0,1:T(2,128)S(1)} %get-tuple-element.681, s32[1024]{0:T(1024)S(1)} %pad_clamp_fusion.26), kind=kCustom, calls=%fused_computation.2.clone.clone.1 | custom fusion | bytes 16779264 | tf_op jit(solution)/shard_map/while/body/eval_jaxpr/jit(_take)/gather | solution.py:129
  563.5 225.8 %while.45 = (s32[]{:T(128)}, f32[2,128,2048]{2,1,0:T(8,128)}, s32[2,4,512]{2,1,0:T(4,128)S(1)}, f32[2,512]{1,0:T(2,128)S(1)}, f32[2,128,2048]{2,0,1:T(2,128)S(1)}, /*index=5*/s32[]{:T(128)}, s32[]{:T(128)}, s32[]{}, s32[]{}, s32[]{}) while((s32[]{:T(128)}, f32[2,128,2048]{2,1,0:T(8,128)}, s32[2,4,512]{2,1,0:T(4,128)S(1)}, ...), condition=%wide.region_3.7_spmd.clone, body=%wide.region_2.6_spmd.clone.sunk | while | flops 3243000320 | bytes 234956048 | solution.py:136
  598.3 30.0 %gather_fusion.4 = f32[512,2,2048]{2,1,0:T(2,128)} fusion(f32[2,128,2048]{2,0,1:T(2,128)S(1)} %get-tuple-element.711, s32[1024]{0:T(1024)S(1)} %pad_clamp_fusion.28), kind=kCustom, calls=%fused_computation.3.clone.clone.1 | custom fusion | bytes 16779264 | tf_op jit(solution)/shard_map/while/body/eval_jaxpr/jit(_take)/gather | solution.py:127
  641.7 19.8 %gather_fusion.5 = f32[512,2,2048]{2,1,0:T(2,128)} fusion(f32[2,128,2048]{2,0,1:T(2,128)S(1)} %get-tuple-element.711, s32[1024]{0:T(1024)S(1)} %pad_clamp_fusion.29), kind=kCustom, calls=%fused_computation.5.clone.clone.1 | custom fusion | bytes 16779264 | tf_op jit(solution)/shard_map/while/body/eval_jaxpr/jit(_take)/gather | solution.py:129
  712.4 19.7 %gather_fusion.4 = f32[512,2,2048]{2,1,0:T(2,128)} fusion(f32[2,128,2048]{2,0,1:T(2,128)S(1)} %get-tuple-element.711, s32[1024]{0:T(1024)S(1)} %pad_clamp_fusion.28), kind=kCustom, calls=%fused_computation.3.clone.clone.1 | custom fusion | bytes 16779264 | tf_op jit(solution)/shard_map/while/body/eval_jaxpr/jit(_take)/gather | solution.py:127
  745.5 19.5 %gather_fusion.5 = f32[512,2,2048]{2,1,0:T(2,128)} fusion(f32[2,128,2048]{2,0,1:T(2,128)S(1)} %get-tuple-element.711, s32[1024]{0:T(1024)S(1)} %pad_clamp_fusion.29), kind=kCustom, calls=%fused_computation.5.clone.clone.1 | custom fusion | bytes 16779264 | tf_op jit(solution)/shard_map/while/body/eval_jaxpr/jit(_take)/gather | solution.py:129
  796.3 30.6 %all_to_all.138 = f32[2,128,2048]{2,0,1:T(2,128)S(1)} all-to-all(f32[2,128,2048]{2,0,1:T(2,128)S(1)} %copy.154), channel_id=1, replica_groups=mesh['mode'=8,'tm'=4] {'mode'}, dimensions={1} | all-to-all | bytes 4194304 | tf_op jit(solution)/shard_map/all_to_all | solution.py:155
  864.2 52.5 %all_to_all.139 = f32[4,1,131072]{2,1,0:T(1,128)} all-to-all(f32[4,1,131072]{2,1,0:T(1,128)S(1)} %reshape.497), channel_id=1, replica_groups=mesh['mode'=8,'tm'=4] {'tm'}, dimensions={0} | all-to-all | bytes 4194304 | tf_op jit(solution)/shard_map/all_to_all | solution.py:69
  970.1 51.0 %all_to_all.140 = f32[4,1,131072]{2,1,0:T(1,128)} all-to-all(f32[4,1,131072]{2,1,0:T(1,128)S(1)} %reshape.499), channel_id=1, replica_groups=mesh['mode'=8,'tm'=4] {'tm'}, dimensions={0} | all-to-all | bytes 4194304 | tf_op jit(solution)/shard_map/all_to_all | solution.py:100
  1081.4 25.5 %collective-permute-done.9 = f32[2,16,2048]{2,1,0:T(8,128)S(1)} collective-permute-done((f32[2,16,2048]{2,1,0:T(8,128)S(1)}, f32[2,16,2048]{2,1,0:T(8,128)S(1)}, u32[]{:S(2)}, u32[]{:S(2)}) %collective-permute-start.9) | collective-permute-done | bytes 262176 | tf_op jit(solution)/shard_map/ppermute | solution.py:147
  1118.3 210.9 %while.46 = (s32[]{:T(128)}, f32[2,128,2048]{2,1,0:T(8,128)}, s32[2,4,512]{2,1,0:T(4,128)S(1)}, f32[2,512]{1,0:T(2,128)S(1)}, f32[2,128,2048]{2,0,1:T(2,128)S(1)}, /*index=5*/s32[]{:T(128)}, s32[]{:T(128)}, s32[]{}, s32[]{}, s32[]{}) while((s32[]{:T(128)}, f32[2,128,2048]{2,1,0:T(8,128)}, s32[2,4,512]{2,1,0:T(4,128)S(1)}, ...), condition=%wide.region_5.9_spmd.clone, body=%wide.region_4.8_spmd.clone.sunk | while | flops 3243000320 | bytes 234956048 | solution.py:136
  1150.5 19.5 %gather_fusion.7 = f32[512,2,2048]{2,1,0:T(2,128)} fusion(f32[2,128,2048]{2,0,1:T(2,128)S(1)} %get-tuple-element.741, s32[1024]{0:T(1024)S(1)} %pad_clamp_fusion.31), kind=kCustom, calls=%fused_computation.6.clone.clone.1 | custom fusion | bytes 16779264 | tf_op jit(solution)/shard_map/while/body/eval_jaxpr/jit(_take)/gather | solution.py:127
  1183.4 19.8 %gather_fusion.8 = f32[512,2,2048]{2,1,0:T(2,128)} fusion(f32[2,128,2048]{2,0,1:T(2,128)S(1)} %get-tuple-element.741, s32[1024]{0:T(1024)S(1)} %pad_clamp_fusion.32), kind=kCustom, calls=%fused_computation.8.clone.clone.1 | custom fusion | bytes 16779264 | tf_op jit(solution)/shard_map/while/body/eval_jaxpr/jit(_take)/gather | solution.py:129
  1222.4 19.3 %gather_fusion.6 = f32[512,2,2048]{2,1,0:T(2,128)} fusion(f32[2,128,2048]{2,0,1:T(2,128)S(1)} %get-tuple-element.741, s32[1024]{0:T(1024)S(1)} %pad_clamp_fusion.30), kind=kCustom, calls=%fused_computation.7.clone.clone.1 | custom fusion | bytes 16779264 | tf_op jit(solution)/shard_map/while/body/eval_jaxpr/jit(_take)/gather | solution.py:128
  1254.1 19.7 %gather_fusion.7 = f32[512,2,2048]{2,1,0:T(2,128)} fusion(f32[2,128,2048]{2,0,1:T(2,128)S(1)} %get-tuple-element.741, s32[1024]{0:T(1024)S(1)} %pad_clamp_fusion.31), kind=kCustom, calls=%fused_computation.6.clone.clone.1 | custom fusion | bytes 16779264 | tf_op jit(solution)/shard_map/while/body/eval_jaxpr/jit(_take)/gather | solution.py:127
  1287.2 19.5 %gather_fusion.8 = f32[512,2,2048]{2,1,0:T(2,128)} fusion(f32[2,128,2048]{2,0,1:T(2,128)S(1)} %get-tuple-element.741, s32[1024]{0:T(1024)S(1)} %pad_clamp_fusion.32), kind=kCustom, calls=%fused_computation.8.clone.clone.1 | custom fusion | bytes 16779264 | tf_op jit(solution)/shard_map/while/body/eval_jaxpr/jit(_take)/gather | solution.py:129
  1333.7 218.8 %while.47 = (s32[]{:T(128)}, f32[2,128,2048]{2,1,0:T(8,128)}, s32[2,4,512]{2,1,0:T(4,128)S(1)}, f32[2,512]{1,0:T(2,128)S(1)}, f32[2,128,2048]{2,0,1:T(2,128)S(1)}, /*index=5*/s32[]{:T(128)}, s32[]{:T(128)}, s32[]{}, s32[]{}, s32[]{}) while((s32[]{:T(128)}, f32[2,128,2048]{2,1,0:T(8,128)}, s32[2,4,512]{2,1,0:T(4,128)S(1)}, ...), condition=%wide.region_7.11_spmd.clone, body=%wide.region_6.10_spmd.clone.sunk | while | flops 3243000320 | bytes 234956048 | solution.py:136
  1368.4 19.8 %gather_fusion.10 = f32[512,2,2048]{2,1,0:T(2,128)} fusion(f32[2,128,2048]{2,0,1:T(2,128)S(1)} %get-tuple-element.771, s32[1024]{0:T(1024)S(1)} %pad_clamp_fusion.34), kind=kCustom, calls=%fused_computation.9.clone.clone.1 | custom fusion | bytes 16779264 | tf_op jit(solution)/shard_map/while/body/eval_jaxpr/jit(_take)/gather | solution.py:127
  1401.6 19.5 %gather_fusion.11 = f32[512,2,2048]{2,1,0:T(2,128)} fusion(f32[2,128,2048]{2,0,1:T(2,128)S(1)} %get-tuple-element.771, s32[1024]{0:T(1024)S(1)} %pad_clamp_fusion.35), kind=kCustom, calls=%fused_computation.11.clone.clone.1 | custom fusion | bytes 16779264 | tf_op jit(solution)/shard_map/while/body/eval_jaxpr/jit(_take)/gather | solution.py:129
  1440.6 19.3 %gather_fusion.9 = f32[512,2,2048]{2,1,0:T(2,128)} fusion(f32[2,128,2048]{2,0,1:T(2,128)S(1)} %get-tuple-element.771, s32[1024]{0:T(1024)S(1)} %pad_clamp_fusion.33), kind=kCustom, calls=%fused_computation.10.clone.clone.1 | custom fusion | bytes 16779264 | tf_op jit(solution)/shard_map/while/body/eval_jaxpr/jit(_take)/gather | solution.py:128
  1472.3 19.5 %gather_fusion.10 = f32[512,2,2048]{2,1,0:T(2,128)} fusion(f32[2,128,2048]{2,0,1:T(2,128)S(1)} %get-tuple-element.771, s32[1024]{0:T(1024)S(1)} %pad_clamp_fusion.34), kind=kCustom, calls=%fused_computation.9.clone.clone.1 | custom fusion | bytes 16779264 | tf_op jit(solution)/shard_map/while/body/eval_jaxpr/jit(_take)/gather | solution.py:127
  1505.2 19.8 %gather_fusion.11 = f32[512,2,2048]{2,1,0:T(2,128)} fusion(f32[2,128,2048]{2,0,1:T(2,128)S(1)} %get-tuple-element.771, s32[1024]{0:T(1024)S(1)} %pad_clamp_fusion.35), kind=kCustom, calls=%fused_computation.11.clone.clone.1 | custom fusion | bytes 16779264 | tf_op jit(solution)/shard_map/while/body/eval_jaxpr/jit(_take)/gather | solution.py:129
  1577.8 20.6 %all-to-all-done.6 = f32[2,128,2048]{2,0,1:T(2,128)S(1)} async-done(((f32[2,128,2048]{2,0,1:T(2,128)}), f32[2,128,2048]{2,0,1:T(2,128)S(1)}, u32[]{:S(2)}, u32[]{:S(2)}) %all-to-all-start.6) | async-done | bytes 2097184 | tf_op jit(solution)/shard_map/all_to_all | solution.py:155
  1657.9 39.8 %all-reduce = (f32[16]{0:T(128)S(1)}, f32[16]{0:T(128)S(1)}, f32[16]{0:T(128)S(1)}, f32[16]{0:T(128)S(1)}) all-reduce(f32[16]{0:T(128)S(1)} %reduce_sum.56, f32[16]{0:T(128)S(1)} %multiply_reduce_fusion, f32[16]{0:T(128)S(1)} %reduce_sum.52, f32[16]{0:T(128)S(1)} %multiply_reduce_fusion.2), channel_id=1, replica_groups=mesh['mode'=8,'tm'=4] {'tm'}, use_global_device_ids=true, to_apply=%region_15.19 | all-reduce | flops 64 | bytes 512 | tf_op jit(solution)/shard_map/psum | solution.py:176
  (437 shorter events, 959.1 us)
Async XLA Ops:
  12.9 50.1 %all-to-all-start = ((f32[4,1,131072]{2,1,0:T(1,128)}), f32[4,1,131072]{2,1,0:T(1,128)S(1)}, u32[]{:S(2)}, u32[]{:S(2)}) async-start(f32[4,1,131072]{2,1,0:T(1,128)} %reshape.491), calls=%async_computation | async-start | bytes 4194304 | tf_op jit(solution)/shard_map/all_to_all | solution.py:42
  18.4 86.5 %copy-start.30 = (f32[256,64]{0,1:T(8,128)}, f32[256,64]{0,1:T(8,128)S(1)}, u32[]{:S(2)}) copy-start(f32[256,64]{0,1:T(8,128)S(1)} %get-tuple-element.449) | copy-start | bytes 196612
  18.4 86.5 %copy-start.32 = (f32[256,64]{0,1:T(8,128)}, f32[256,64]{0,1:T(8,128)S(1)}, u32[]{:S(2)}) copy-start(f32[256,64]{0,1:T(8,128)S(1)} %get-tuple-element.450) | copy-start | bytes 196612
  110.5 13.2 copy-start.43
  116.1 52.2 %all-to-all-start.1 = ((f32[4,1,131072]{2,1,0:T(1,128)}), f32[4,1,131072]{2,1,0:T(1,128)}, u32[]{:S(2)}, u32[]{:S(2)}) async-start(f32[4,1,131072]{2,1,0:T(1,128)} %reshape.493), calls=%async_computation.1 | async-start | bytes 4194304 | tf_op jit(solution)/shard_map/all_to_all | solution.py:69
  123.8 74.3 %copy-start.36 = (f32[16]{0:T(128)}, f32[16]{0:T(128)S(1)}, u32[]{:S(2)}) copy-start(f32[16]{0:T(128)S(1)} %get-tuple-element.443) | copy-start | bytes 196
  123.8 74.3 %copy-start.38 = (f32[16]{0:T(128)}, f32[16]{0:T(128)S(1)}, u32[]{:S(2)}) copy-start(f32[16]{0:T(128)S(1)} %get-tuple-element.444) | copy-start | bytes 196
  123.8 74.3 %copy-start.40 = (f32[16]{0:T(128)}, f32[16]{0:T(128)S(1)}, u32[]{:S(2)}) copy-start(f32[16]{0:T(128)S(1)} %get-tuple-element.445) | copy-start | bytes 196
  124.2 74.0 %copy-start.28 = (f32[64,256]{1,0:T(8,128)}, f32[64,256]{1,0:T(8,128)S(1)}, u32[]{:S(2)}) copy-start(f32[64,256]{1,0:T(8,128)S(1)} %get-tuple-element.448) | copy-start | bytes 196612
  124.2 86.1 %copy-start.24 = (f32[64,256]{1,0:T(8,128)}, f32[64,256]{1,0:T(8,128)S(1)}, u32[]{:S(2)}) copy-start(f32[64,256]{1,0:T(8,128)S(1)} %get-tuple-element.446) | copy-start | bytes 196612
  124.2 86.1 %copy-start.26 = (f32[64,256]{1,0:T(8,128)}, f32[64,256]{1,0:T(8,128)S(1)}, u32[]{:S(2)}) copy-start(f32[64,256]{1,0:T(8,128)S(1)} %get-tuple-element.447) | copy-start | bytes 196612
  222.6 52.3 %all-to-all-start.2 = ((f32[4,1,131072]{2,1,0:T(1,128)}), f32[4,1,131072]{2,1,0:T(1,128)}, u32[]{:S(2)}, u32[]{:S(2)}) async-start(f32[4,1,131072]{2,1,0:T(1,128)} %reshape.495), calls=%async_computation.2 | async-start | bytes 4194304 | tf_op jit(solution)/shard_map/all_to_all | solution.py:100
  318.7 6.9 collective-permute-start
  318.7 14.0 collective-permute-start.1
  320.5 17.5 %collective-permute-start.2 = (f32[2,16,2048]{2,1,0:T(8,128)S(1)}, f32[2,16,2048]{2,1,0:T(8,128)S(1)}, u32[]{:S(2)}, u32[]{:S(2)}) collective-permute-start(f32[2,16,2048]{2,1,0:T(8,128)S(1)} %get-tuple-element.440), channel_id=1, source_target_pairs={{0,20},{4,24},{8,28},{12,0},{16,4},{20,8},{24,12},{28,16},{1,21},{... | collective-permute-start | bytes 786440 | tf_op jit(solution)/shard_map/ppermute | solution.py:147
  320.7 23.8 %collective-permute-start.3 = (f32[2,16,2048]{2,1,0:T(8,128)S(1)}, f32[2,16,2048]{2,1,0:T(8,128)S(1)}, u32[]{:S(2)}, u32[]{:S(2)}) collective-permute-start(f32[2,16,2048]{2,1,0:T(8,128)S(1)} %get-tuple-element.439), channel_id=1, source_target_pairs={{0,16},{4,20},{8,24},{12,28},{16,0},{20,4},{24,8},{28,12},{1,17},{... | collective-permute-start | bytes 786440 | tf_op jit(solution)/shard_map/ppermute | solution.py:147
  321.3 23.4 %collective-permute-start.4 = (f32[2,16,2048]{2,1,0:T(8,128)S(1)}, f32[2,16,2048]{2,1,0:T(8,128)S(1)}, u32[]{:S(2)}, u32[]{:S(2)}) collective-permute-start(f32[2,16,2048]{2,1,0:T(8,128)S(1)} %get-tuple-element.438), channel_id=1, source_target_pairs={{0,12},{4,16},{8,20},{12,24},{16,28},{20,0},{24,4},{28,8},{1,13},{... | collective-permute-start | bytes 786440 | tf_op jit(solution)/shard_map/ppermute | solution.py:147
  325.6 19.0 %collective-permute-start.5 = (f32[2,16,2048]{2,1,0:T(8,128)S(1)}, f32[2,16,2048]{2,1,0:T(8,128)S(1)}, u32[]{:S(2)}, u32[]{:S(2)}) collective-permute-start(f32[2,16,2048]{2,1,0:T(8,128)S(1)} %get-tuple-element.437), channel_id=1, source_target_pairs={{0,8},{4,12},{8,16},{12,20},{16,24},{20,28},{24,0},{28,4},{1,9},{5... | collective-permute-start | bytes 786440 | tf_op jit(solution)/shard_map/ppermute | solution.py:147
  332.8 12.0 collective-permute-start.6
  839.0 11.7 copy-start.33
  1064.7 14.6 collective-permute-start.7
  1064.7 15.6 collective-permute-start.8
  1069.9 490.8 %all-to-all-start.8 = ((f32[2,128,2048]{2,0,1:T(2,128)}), f32[2,128,2048]{2,0,1:T(2,128)}, u32[]{:S(2)}, u32[]{:S(2)}) async-start(f32[2,128,2048]{2,0,1:T(2,128)} %copy.173), calls=%async_computation.8 | async-start | bytes 4194304 | tf_op jit(solution)/shard_map/all_to_all | solution.py:156
  1075.4 31.5 %collective-permute-start.9 = (f32[2,16,2048]{2,1,0:T(8,128)S(1)}, f32[2,16,2048]{2,1,0:T(8,128)S(1)}, u32[]{:S(2)}, u32[]{:S(2)}) collective-permute-start(f32[2,16,2048]{2,1,0:T(8,128)S(1)} %get-tuple-element.431), channel_id=1, source_target_pairs={{0,20},{4,24},{8,28},{12,0},{16,4},{20,8},{24,12},{28,16},{1,21},{... | collective-permute-start | bytes 786440 | tf_op jit(solution)/shard_map/ppermute | solution.py:147
  1076.7 38.0 %collective-permute-start.10 = (f32[2,16,2048]{2,1,0:T(8,128)S(1)}, f32[2,16,2048]{2,1,0:T(8,128)S(1)}, u32[]{:S(2)}, u32[]{:S(2)}) collective-permute-start(f32[2,16,2048]{2,1,0:T(8,128)S(1)} %get-tuple-element.430), channel_id=1, source_target_pairs={{0,16},{4,20},{8,24},{12,28},{16,0},{20,4},{24,8},{28,12},{1,17},{... | collective-permute-start | bytes 786440 | tf_op jit(solution)/shard_map/ppermute | solution.py:147
  1077.2 37.4 %collective-permute-start.11 = (f32[2,16,2048]{2,1,0:T(8,128)S(1)}, f32[2,16,2048]{2,1,0:T(8,128)S(1)}, u32[]{:S(2)}, u32[]{:S(2)}) collective-permute-start(f32[2,16,2048]{2,1,0:T(8,128)S(1)} %get-tuple-element.429), channel_id=1, source_target_pairs={{0,12},{4,16},{8,20},{12,24},{16,28},{20,0},{24,4},{28,8},{1,13},{... | collective-permute-start | bytes 786440 | tf_op jit(solution)/shard_map/ppermute | solution.py:147
  1079.3 35.4 %collective-permute-start.12 = (f32[2,16,2048]{2,1,0:T(8,128)S(1)}, f32[2,16,2048]{2,1,0:T(8,128)S(1)}, u32[]{:S(2)}, u32[]{:S(2)}) collective-permute-start(f32[2,16,2048]{2,1,0:T(8,128)S(1)} %get-tuple-element.428), channel_id=1, source_target_pairs={{0,8},{4,12},{8,16},{12,20},{16,24},{20,28},{24,0},{28,4},{1,9},{5... | collective-permute-start | bytes 786440 | tf_op jit(solution)/shard_map/ppermute | solution.py:147
  1080.3 34.4 %collective-permute-start.13 = (f32[2,16,2048]{2,1,0:T(8,128)S(1)}, f32[2,16,2048]{2,1,0:T(8,128)S(1)}, u32[]{:S(2)}, u32[]{:S(2)}) collective-permute-start(f32[2,16,2048]{2,1,0:T(8,128)S(1)} %get-tuple-element.427), channel_id=1, source_target_pairs={{0,4},{4,8},{8,12},{12,16},{16,20},{20,24},{24,28},{28,0},{1,5},{5... | collective-permute-start | bytes 786440 | tf_op jit(solution)/shard_map/ppermute | solution.py:147
  1560.7 37.7 %all-to-all-start.6 = ((f32[2,128,2048]{2,0,1:T(2,128)}), f32[2,128,2048]{2,0,1:T(2,128)S(1)}, u32[]{:S(2)}, u32[]{:S(2)}) async-start(f32[2,128,2048]{2,0,1:T(2,128)} %copy.168), calls=%async_computation.6 | async-start | bytes 4194304 | tf_op jit(solution)/shard_map/all_to_all | solution.py:155
  1598.4 31.0 %all-to-all-start.9 = ((f32[2,128,2048]{2,0,1:T(2,128)}), f32[2,128,2048]{2,0,1:T(2,128)}, u32[]{:S(2)}, u32[]{:S(2)}) async-start(f32[2,128,2048]{2,0,1:T(2,128)} %copy.174), calls=%async_computation.9 | async-start | bytes 4194304 | tf_op jit(solution)/shard_map/all_to_all | solution.py:156
  1623.7 27.3 %copy-start.16 = (f32[2,128,2048]{2,0,1:T(2,128)S(1)}, f32[2,128,2048]{2,0,1:T(2,128)}, u32[]{:S(2)}) copy-start(f32[2,128,2048]{2,0,1:T(2,128)} %copy-done.15) | copy-start | bytes 6291460
  1629.4 68.9 %all-to-all-start.7 = ((f32[4,1,131072]{2,1,0:T(1,128)}), f32[4,1,131072]{2,1,0:T(1,128)}, u32[]{:S(2)}, u32[]{:S(2)}) async-start(f32[4,1,131072]{2,1,0:T(1,128)} %reshape.501), calls=%async_computation.7 | async-start | bytes 4194304 | tf_op jit(solution)/shard_map/all_to_all | solution.py:46
  (45 other events, 331.2 us)
